TPU v7x, 128 devices: a whole 4x4x4 slice. The times are simulated.
128 devices in a mesh: role: 2 (over core), tok: 64 (over y, x, z).
Axes of the slice: x: 4, y: 4, z: 4, core: 2. Of those that a mesh axis runs over, the one named last changes fastest.
Arguments:
- hidden: bfloat16 [16384, 2048], P('tok'), may hold values from -6 to 6
- doc_blocks: int32 [10], replicated, may hold values from 1 to 16, 128 in all
- norm_gain: float32 [2048], replicated, may hold values from 0.5 to 2
- w_query: bfloat16 [2048, 4096], P(None, 'role'), may hold values from -0.125 to 0.125
- w_key: bfloat16 [2048, 512], P(None, 'role'), may hold values from -0.125 to 0.125
- w_value: bfloat16 [2048, 512], P(None, 'role'), may hold values from -0.125 to 0.125
- q_gain: float32 [128], replicated, may hold values from 0.5 to 6
- k_gain: float32 [128], replicated, may hold values from 0.5 to 6
- w_out: bfloat16 [4096, 2048], P('role'), may hold values from -0.09375 to 0.09375
Outputs:
- attn_out: bfloat16 [16384, 2048], P('tok', 'role')
All inputs are finite; a program needn't handle non-finite values.
Results may differ from a plain program's by a relative error of at most 0.006.
The roundings to bfloat16 on the way count: a program that leaves them out, or rounds other values in their place, can miss the bound.
Values may be sent and summed in bfloat16 or wider, within the bound.
No kernel may reach another device: no remote copies, remote signals or barrier semaphores. Data moves between devices by JAX's collectives and lax.ppermute only.
A program may use at most 192 MiB of HBM per device.

v0:
```python
import functools

import numpy as np
import jax
import jax.numpy as jnp
from jax import lax
from jax.experimental import pallas as pl
from jax.experimental.pallas import tpu as pltpu
from jax.sharding import PartitionSpec as P

HD = 128
BLK = 128
NDOCS = 10
EPSILON = 1e-06
THETA = 1000000.0
TOK = 256
RING = 4
EXTRA = 16
AHEAD = 3
QBLOCKS = 8
BF = jnp.bfloat16
F32 = jnp.float32
SCALE2 = float(HD ** (-0.5) * np.log2(np.e))


def doc_start(docs, block):
    end = jnp.int32(0)
    start = jnp.int32(0)
    for j in range(NDOCS):
        end = end + docs[j]
        start = jnp.where(end <= block, end, start)
    return start


def head_norm_rope(x, gain, cos, sin):
    ms = jnp.mean(x * x, axis=-1, keepdims=True)
    x = x * lax.rsqrt(ms + EPSILON) * gain
    return (x * cos + pltpu.roll(x, HD // 2, 1) * sin).astype(BF)


def head_norm_rope_t(x, gain, cos, sin):
    ms = jnp.mean(x * x, axis=0, keepdims=True)
    x = x * lax.rsqrt(ms + EPSILON) * gain
    turned = jnp.concatenate([x[HD // 2:], x[:HD // 2]], axis=0)
    return (x * cos + turned * sin).astype(BF)


def fetch(pairs, sems):
    copies = [pltpu.make_async_copy(src, dst, sems.at[n]) for n, (src, dst) in enumerate(pairs)]
    for c in copies:
        c.start()
    return copies


def kv_kernel(docs, hid, ngain, wk, wv, kgain, freq, normed_o, kv_o, cos_o, sin_o,
              hid_b, ngain_b, wk_b, wv_b, kgain_b, freq_b, sems):
    copies = fetch(((freq, freq_b), (ngain, ngain_b), (kgain, kgain_b), (hid, hid_b),
                    (wk, wk_b), (wv, wv_b)), sems)
    first = lax.axis_index("tok") * 2
    s0 = doc_start(docs, first) * BLK
    s1 = doc_start(docs, first + 1) * BLK
    row = lax.broadcasted_iota(jnp.int32, (TOK, HD), 0)
    pos = first * BLK + row - jnp.where(row < BLK, s0, s1)
    for c in copies[:3]:
        c.wait()
    ang = pos.astype(F32) * freq_b[...]
    cos = jnp.cos(ang)
    lane = lax.broadcasted_iota(jnp.int32, (TOK, HD), 1)
    sin = jnp.sin(ang)
    sin = jnp.where(lane < HD // 2, -sin, sin)
    cos_o[...] = cos.T
    sin_o[...] = sin.T
    copies[3].wait()
    x = hid_b[...].astype(F32)
    ms = jnp.mean(x * x, axis=-1, keepdims=True)
    normed = (x * lax.rsqrt(ms + EPSILON) * ngain_b[...]).astype(BF)
    normed_o[...] = normed
    copies[4].wait()
    k = jnp.dot(normed, wk_b[...], preferred_element_type=F32)
    copies[5].wait()
    v = jnp.dot(normed, wv_b[...], preferred_element_type=F32)
    for h in range(2):
        kv_o[0, :, h * HD:(h + 1) * HD] = head_norm_rope(
            k[:, h * HD:(h + 1) * HD], kgain_b[...], cos, sin)
    kv_o[1] = v.T.astype(BF)


def q_kernel(normed, wq, qgain, cos, sin, q_o, wq_b, acc, qgain_b, sems):
    depth = wq.shape[0]
    rows = depth // QBLOCKS
    copies = fetch([(qgain, qgain_b)] + [
        (wq.at[b * rows:(b + 1) * rows], wq_b.at[b * rows:(b + 1) * rows])
        for b in range(QBLOCKS)], sems)
    half = depth // 2
    width = 2 * HD
    blocks = wq.shape[1] // width
    for c in copies[:1 + QBLOCKS // 2]:
        c.wait()
    gain = jnp.broadcast_to(qgain_b[...], (TOK, HD)).T
    for b in range(blocks):
        cols = slice(b * width, (b + 1) * width)
        acc[:, cols] = jnp.dot(normed[:, :half], wq_b[:half, cols], preferred_element_type=F32)
    for c in copies[1 + QBLOCKS // 2:]:
        c.wait()
    for b in range(blocks):
        cols = slice(b * width, (b + 1) * width)
        q = acc[:, cols] + jnp.dot(normed[:, half:], wq_b[half:, cols], preferred_element_type=F32)
        for h in range(2):
            q_o[2 * b + h] = head_norm_rope_t(
                q[:, h * HD:(h + 1) * HD].T, gain, cos[...], sin[...])


def attend_kernel(table, first_stage, last_stage, *refs):
    slots = len(table)
    refs = list(refs)
    docs, q = refs[:2]
    refs = refs[2:]
    pieces, refs = list(refs[:slots]), refs[slots:]
    me = lax.axis_index("tok")
    role = lax.axis_index("role")
    if first_stage:
        own, refs = refs[0], refs[1:]
    else:
        m_in, acc_in = refs[:2]
        refs = refs[2:]
    if last_stage:
        wout, refs = refs[0], refs[1:]
        send_o, keep_o, win, hops, m_s, acc_s, att = refs
    else:
        m_s, acc_s, win, hops = refs
    sources = pieces + ([own] if first_stage else [])
    for n, piece in enumerate(sources):
        win[n] = piece[...]
    if not first_stage:
        m_s[...] = m_in[...]
        acc_s[...] = acc_in[...]
    z = me % RING
    for n, row in enumerate(table):
        hop = jnp.int32(row[0])
        for zz in range(1, RING):
            hop = jnp.where(z == zz, jnp.int32(row[zz]), hop)
        hops[n] = hop
    step = 2 * BLK

    def tile(i, slot, lo, size, mask, first):
        units = [(g, j) for g in range(2) for j in range(4)]

        def scores(g, j):
            k = win[slot, 0, lo:lo + size, g * HD:(g + 1) * HD]
            qt = jnp.concatenate(
                [q[g * 8 + 2 * j + e, :, i * BLK:(i + 1) * BLK] for e in range(2)], axis=1)
            s = jnp.dot(k, qt, preferred_element_type=F32)
            return s if mask is None else jnp.where(mask, s, -1e30)

        ahead = [scores(*units[n]) for n in range(AHEAD)]
        for n, (g, j) in enumerate(units):
            s = ahead.pop(0)
            if n + AHEAD < len(units):
                ahead.append(scores(*units[n + AHEAD]))
            cols = slice(j * step, (j + 1) * step)
            v = win[slot, 1, g * HD:(g + 1) * HD, lo:lo + size]
            v1 = jnp.concatenate([v, jnp.ones((EXTRA, size), BF)], axis=0)
            top = jnp.max(s, axis=0, keepdims=True)
            if first:
                m_new = top
            else:
                m_old = m_s[i, g, :, cols]
                m_new = jnp.maximum(m_old, top)
            p = jnp.exp2((s - m_new) * SCALE2).astype(BF)
            pv = jnp.dot(v1, p, preferred_element_type=F32)
            if first:
                acc_s[i, g, :, cols] = pv
            else:
                acc_s[i, g, :, cols] = acc_s[i, g, :, cols] * jnp.exp2((m_old - m_new) * SCALE2) + pv
            m_s[i, g, :, cols] = m_new

    for i in range(2):
        block = me * 2 + i
        depth = block - doc_start(docs, block)
        if first_stage:
            size = BLK * (i + 1)
            key = lax.broadcasted_iota(jnp.int32, (size, step), 0)
            token = lax.broadcasted_iota(jnp.int32, (size, step), 1) % BLK
            mask = key <= token + i * BLK
            if i == 1:
                mask = mask & (key >= jnp.where(depth == 0, BLK, 0))
            tile(i, slots, 0, size, mask, True)

        @pl.loop(0, slots)
        def _(slot):
            hop = hops[slot]

            @pl.when((hop > 0) & (2 * hop + i <= depth))
            def _():
                tile(i, slot, 0, 2 * BLK, None, False)

            @pl.when((hop > 0) & (2 * hop + i == depth + 1))
            def _():
                tile(i, slot, BLK, BLK, None, False)

        if last_stage:
            for g in range(2):
                for h in range(8):
                    cols = slice(h * BLK, (h + 1) * BLK)
                    o = acc_s[i, g, :HD, cols] * (1.0 / acc_s[i, g, HD:HD + 1, cols])
                    att[i * BLK:(i + 1) * BLK, (g * 8 + h) * HD:(g * 8 + h + 1) * HD] = o.T.astype(BF)
    if last_stage:
        half = wout.shape[1] // 2
        a = att[...]
        theirs = pl.multiple_of((1 - role) * half, half)
        mine = pl.multiple_of(role * half, half)
        send_o[...] = jnp.dot(a, wout[:, pl.ds(theirs, half)], preferred_element_type=F32).astype(BF)
        keep_o[...] = jnp.dot(a, wout[:, pl.ds(mine, half)], preferred_element_type=F32)


HBM = pl.BlockSpec(memory_space=pltpu.MemorySpace.HBM)
SMEM = pl.BlockSpec(memory_space=pltpu.MemorySpace.SMEM)
VM = pl.BlockSpec(memory_space=pltpu.MemorySpace.VMEM)


def shifted(value, by):
    peers = lax.axis_size("tok")
    return lax.ppermute(value, "tok", [(t, (t + by) % peers) for t in range(peers)])


def moved(value, rows, turn, senders=(0, 1, 2, 3)):
    peers = lax.axis_size("tok")
    pairs = []
    for t in range(peers):
        z = t % RING
        if z in senders:
            pairs.append((t, (t - z + (z + turn) % RING + rows * RING) % peers))
    return lax.ppermute(value, "tok", pairs)


NEAR = ((4, 4, 4, 4), (0, 1, 1, 1), (0, 0, 0, 3), (8, 8, 8, 8))
MID = ((1, 5, 5, 5), (3, 3, 3, 7), (2, 2, 6, 6))
FAR = ((6, 6, 2, 2), (7, 7, 7, 0), (5, 0, 0, 0))


def layer(hidden, doc_blocks, norm_gain, w_query, w_key, w_value, q_gain, k_gain, w_out):
    d = hidden.shape[1]
    hq = w_query.shape[1] // HD
    freq = THETA ** (-(np.arange(HD // 2, dtype=np.float32) * np.float32(2.0)) / np.float32(HD))
    freq = jnp.asarray(np.concatenate([freq, freq])[None].astype(np.float32))
    doc_blocks, hidden, norm_row, w_key, w_value, k_row, freq, q_row, w_query = (
        pltpu.with_memory_space_constraint(x, pltpu.MemorySpace.HBM)
        for x in (doc_blocks, hidden, norm_gain[None], w_key, w_value, k_gain[None], freq, q_gain[None], w_query))
    normed, kv, cos, sin = pl.pallas_call(
        kv_kernel,
        out_shape=(
            jax.ShapeDtypeStruct((TOK, d), BF),
            jax.ShapeDtypeStruct((2, TOK, 2 * HD), BF),
            jax.ShapeDtypeStruct((HD, TOK), F32),
            jax.ShapeDtypeStruct((HD, TOK), F32),
        ),
        in_specs=[SMEM] + [HBM] * 6,
        out_specs=[VM] * 4,
        scratch_shapes=[
            pltpu.VMEM((TOK, d), BF),
            pltpu.VMEM((1, d), F32),
            pltpu.VMEM(w_key.shape, BF),
            pltpu.VMEM(w_value.shape, BF),
            pltpu.VMEM((1, HD), F32),
            pltpu.VMEM((1, HD), F32),
            pltpu.SemaphoreType.DMA((6,)),
        ],
        cost_estimate=pl.CostEstimate(flops=540_000_000, transcendentals=0, bytes_accessed=4_000_000),
        name="kv_kernel",
        compiler_params=pltpu.CompilerParams(vmem_limit_bytes=16 << 20),
    )(doc_blocks, hidden, norm_row, w_key, w_value, k_row, freq)

    row1 = shifted(kv, RING)
    up1 = moved(kv, 0, 1)
    down1 = moved(kv, 0, -1)
    row2 = shifted(kv, 2 * RING)

    queries = pl.pallas_call(
        q_kernel,
        out_shape=jax.ShapeDtypeStruct((hq, HD, TOK), BF),
        in_specs=[VM, HBM, HBM, VM, VM],
        out_specs=VM,
        scratch_shapes=[
            pltpu.VMEM(w_query.shape, BF),
            pltpu.VMEM((TOK, w_query.shape[1]), F32),
            pltpu.VMEM((1, HD), F32),
            pltpu.SemaphoreType.DMA((QBLOCKS + 1,)),
        ],
        cost_estimate=pl.CostEstimate(flops=2_147_000_000, transcendentals=0, bytes_accessed=10_000_000),
        name="q_kernel",
        compiler_params=pltpu.CompilerParams(vmem_limit_bytes=24 << 20),
    )(normed, w_query, q_row, cos, sin)

    lower = lax.axis_index("tok") % RING < RING // 2
    mid = [shifted(up1, RING)]
    mid.append(shifted(down1, RING))
    mid.append(moved(row1, 0, 2))
    mixed = jnp.where(lower, kv, row2)
    far = [moved(mixed, 0, 2)]
    far.append(moved(row2, 0, -1, (1, 2, 3)))
    far.append(moved(row2, 0, 1, (3,)))
    state = (
        jax.ShapeDtypeStruct((2, 2, 1, 8 * BLK), F32),
        jax.ShapeDtypeStruct((2, 2, HD + EXTRA, 8 * BLK), F32),
    )

    def stage(table, operands, extra):
        return pl.pallas_call(
            functools.partial(attend_kernel, table, extra, False),
            out_shape=state,
            in_specs=[SMEM] + [VM] * (len(operands) + 1),
            out_specs=[VM, VM],
            scratch_shapes=[
                pltpu.VMEM((len(table) + extra, 2, TOK, 2 * HD), BF),
                pltpu.SMEM((len(table),), jnp.int32),
            ],
            cost_estimate=pl.CostEstimate(flops=6_000_000_000, transcendentals=0, bytes_accessed=6_000_000),
            compiler_params=pltpu.CompilerParams(vmem_limit_bytes=24 << 20),
        )(doc_blocks, queries, *operands)

    partial = stage(NEAR, [row1, up1, down1, row2, kv], True)
    partial = stage(MID, [*mid, *partial], False)
    half = w_out.shape[1] // 2
    send, keep = pl.pallas_call(
        functools.partial(attend_kernel, FAR, False, True),
        out_shape=(
            jax.ShapeDtypeStruct((TOK, half), BF),
            jax.ShapeDtypeStruct((TOK, half), F32),
        ),
        in_specs=[SMEM] + [VM] * (len(FAR) + 4),
        out_specs=[VM, VM],
        scratch_shapes=[
            pltpu.VMEM((len(FAR), 2, TOK, 2 * HD), BF),
            pltpu.SMEM((len(FAR),), jnp.int32),
            pltpu.VMEM(state[0].shape, F32),
            pltpu.VMEM(state[1].shape, F32),
            pltpu.VMEM((TOK, hq * HD), BF),
        ],
        cost_estimate=pl.CostEstimate(flops=9_000_000_000, transcendentals=0, bytes_accessed=14_000_000),
        name="attend_far",
        compiler_params=pltpu.CompilerParams(vmem_limit_bytes=28 << 20),
    )(doc_blocks, queries, *far, *partial, w_out)
    other = lax.ppermute(send, "role", [(0, 1), (1, 0)])
    return (keep + other.astype(F32)).astype(BF)


def solution(mesh):
    return jax.shard_map(
        layer,
        mesh=mesh,
        in_specs=(
            P("tok", None), P(), P(), P(None, "role"), P(None, "role"), P(None, "role"),
            P(), P(), P("role", None),
        ),
        out_specs=P("tok", "role"),
        check_vma=False,
    )
```

profile of v0, /device:TPU:1, one launch (start us, length us, event | category | flops | bytes accessed | tf_op | source)
XLA Modules:
  0.0 51.4 jit_solution(14810489113175097079)
XLA Ops:
  0.0 3.9 %kv_kernel.1 = (bf16[256,2048]{1,0:T(8,128)(2,1)S(1)}, bf16[2,256,256]{2,1,0:T(8,128)(2,1)S(1)}, f32[128,256]{1,0:T(8,128)S(1)}, f32[128,256]{1,0:T(8,128)S(1)}) custom-call(s32[10]{0:T(128)} %refs_0_.5, bf16[256,2048]{1,0:T(8,128)(2,1)} %hid.1, f32[1,2048]{1,0:T(1,128)} %bitcast.5, bf16[2048,256]{1,0:T(8,128)(2,1)} %wk.1, bf16[2048,256]{1,0:T(8,128)(2,1)} %wv.1, ...), custom_call_target="tpu_custom_call" | custom-call | flops 540000000 | bytes 4000000 | tf_op jit(solution)/shard_map/kv_kernel/pallas_call | solution.py:249
  3.9 3.6 %collective-permute-start = (bf16[2,256,256]{2,1,0:T(8,128)(2,1)S(1)}, bf16[2,256,256]{2,1,0:T(8,128)(2,1)S(1)}, u32[]{:S(2)}, u32[]{:S(2)}) collective-permute-start(bf16[2,256,256]{2,1,0:T(8,128)(2,1)S(1)} %get-tuple-element.18.refs_6_), channel_id=1, source_target_pairs={{0,8},{1,9},{2,10},{3,11},{4,12},{5,13},{6,14},{7,15},{8,16},{9,17... | collective-permute-start | bytes 786440 | tf_op jit(solution)/shard_map/ppermute | solution.py:223
  7.6 1.6 %collective-permute-start.4 = (bf16[2,256,256]{2,1,0:T(8,128)(2,1)S(1)}, bf16[2,256,256]{2,1,0:T(8,128)(2,1)S(1)}, u32[]{:S(2)}, u32[]{:S(2)}) collective-permute-start(bf16[2,256,256]{2,1,0:T(8,128)(2,1)S(1)} %get-tuple-element.18.refs_6_), channel_id=1, source_target_pairs={{0,1},{1,2},{2,3},{3,0},{4,5},{5,6},{6,7},{7,4},{8,9},{9,10},{10,1... | collective-permute-start | bytes 786440 | tf_op jit(solution)/shard_map/ppermute | solution.py:233
  9.2 2.1 %collective-permute-start.6 = (bf16[2,256,256]{2,1,0:T(8,128)(2,1)S(1)}, bf16[2,256,256]{2,1,0:T(8,128)(2,1)S(1)}, u32[]{:S(2)}, u32[]{:S(2)}) collective-permute-start(bf16[2,256,256]{2,1,0:T(8,128)(2,1)S(1)} %get-tuple-element.18.refs_6_), channel_id=1, source_target_pairs={{0,3},{1,0},{2,1},{3,2},{4,7},{5,4},{6,5},{7,6},{8,11},{9,8},{10,9... | collective-permute-start | bytes 786440 | tf_op jit(solution)/shard_map/ppermute | solution.py:233
  11.3 0.3 collective-permute-start.8
  11.6 5.1 %q_kernel.1.refs_1_ = bf16[16,128,256]{2,1,0:T(8,128)(2,1)S(1)} custom-call(bf16[256,2048]{1,0:T(8,128)(2,1)S(1)} %get-tuple-element.15.normed, bf16[2048,2048]{1,0:T(8,128)(2,1)} %wq.1, f32[1,128]{1,0:T(1,128)} %bitcast.7, f32[128,256]{1,0:T(8,128)S(1)} %get-tuple-element.16.cos, f32[128,256]{1,0:T(8,128)S(1)} %get-tuple-element.17.sin), custom_call_target="tpu_custom_call" | custom-call | flops 2147000064 | bytes 10000000 | tf_op jit(solution)/shard_map/q_kernel/pallas_call | solution.py:278
  16.8 0.0 collective-permute-done.refs_5_
  16.9 2.7 %collective-permute-start.1 = (bf16[2,256,256]{2,1,0:T(8,128)(2,1)S(1)}, bf16[2,256,256]{2,1,0:T(8,128)(2,1)S(1)}, u32[]{:S(2)}, u32[]{:S(2)}) collective-permute-start(bf16[2,256,256]{2,1,0:T(8,128)(2,1)S(1)} %broadcast_select_fusion), channel_id=1, source_target_pairs={{0,2},{1,3},{2,0},{3,1},{4,6},{5,7},{6,4},{7,5},{8,10},{9,11},{10,... | collective-permute-start | bytes 786440 | tf_op jit(solution)/shard_map/ppermute | solution.py:233
  19.6 1.3 %collective-permute-start.2 = (bf16[2,256,256]{2,1,0:T(8,128)(2,1)S(1)}, bf16[2,256,256]{2,1,0:T(8,128)(2,1)S(1)}, u32[]{:S(2)}, u32[]{:S(2)}) collective-permute-start(bf16[2,256,256]{2,1,0:T(8,128)(2,1)S(1)} %collective-permute-done.refs_5_), channel_id=1, source_target_pairs={{1,0},{2,1},{3,2},{5,4},{6,5},{7,6},{9,8},{10,9},{11,10},{13,12},{... | collective-permute-start | bytes 786440 | tf_op jit(solution)/shard_map/ppermute | solution.py:233
  20.9 0.0 collective-permute-done.4.refs_3_
  20.9 1.0 %collective-permute-start.5 = (bf16[2,256,256]{2,1,0:T(8,128)(2,1)S(1)}, bf16[2,256,256]{2,1,0:T(8,128)(2,1)S(1)}, u32[]{:S(2)}, u32[]{:S(2)}) collective-permute-start(bf16[2,256,256]{2,1,0:T(8,128)(2,1)S(1)} %collective-permute-done.4.refs_3_), channel_id=1, source_target_pairs={{0,4},{1,5},{2,6},{3,7},{4,8},{5,9},{6,10},{7,11},{8,12},{9,13},{1... | collective-permute-start | bytes 786440 | tf_op jit(solution)/shard_map/ppermute | solution.py:223
  21.9 0.0 collective-permute-done.6.refs_4_
  21.9 0.1 collective-permute-start.7
  22.0 0.0 collective-permute-done.8.refs_2_
  22.0 3.5 %collective-permute-start.9 = (bf16[2,256,256]{2,1,0:T(8,128)(2,1)S(1)}, bf16[2,256,256]{2,1,0:T(8,128)(2,1)S(1)}, u32[]{:S(2)}, u32[]{:S(2)}) collective-permute-start(bf16[2,256,256]{2,1,0:T(8,128)(2,1)S(1)} %collective-permute-done.8.refs_2_), channel_id=1, source_target_pairs={{0,2},{1,3},{2,0},{3,1},{4,6},{5,7},{6,4},{7,5},{8,10},{9,11},{10,... | collective-permute-start | bytes 786440 | tf_op jit(solution)/shard_map/ppermute | solution.py:233
  25.5 0.0 slice-start
  25.5 2.7 %shard_map.100 = (f32[2,2,1,1024]{3,2,1,0:T(1,128)S(1)}, f32[2,2,144,1024]{3,2,1,0:T(8,128)S(1)}) custom-call(s32[10]{0:T(128)} %refs_0_.5, bf16[16,128,256]{2,1,0:T(8,128)(2,1)S(1)} %q_kernel.1.refs_1_, bf16[2,256,256]{2,1,0:T(8,128)(2,1)S(1)} %collective-permute-done.8.refs_2_, bf16[2,256,256]{2,1,0:T(8,128)(2,1)S(1)} %collective-permute-done.4.refs_3_, ...), custom_call_target="tpu_custom_call" | custom-call | flops 6000000000 | bytes 6000000 | tf_op jit(solution)/shard_map/pallas_call | solution.py:308
  28.2 1.3 %collective-permute-done.5.refs_2_ = bf16[2,256,256]{2,1,0:T(8,128)(2,1)S(1)} collective-permute-done((bf16[2,256,256]{2,1,0:T(8,128)(2,1)S(1)}, bf16[2,256,256]{2,1,0:T(8,128)(2,1)S(1)}, u32[]{:S(2)}, u32[]{:S(2)}) %collective-permute-start.5) | collective-permute-done | bytes 262176 | tf_op jit(solution)/shard_map/ppermute | solution.py:223
  29.5 1.5 %collective-permute-start.3 = (bf16[2,256,256]{2,1,0:T(8,128)(2,1)S(1)}, bf16[2,256,256]{2,1,0:T(8,128)(2,1)S(1)}, u32[]{:S(2)}, u32[]{:S(2)}) collective-permute-start(bf16[2,256,256]{2,1,0:T(8,128)(2,1)S(1)} %collective-permute-done.refs_5_), channel_id=1, source_target_pairs={{3,0},{7,4},{11,8},{15,12},{19,16},{23,20},{27,24},{31,28},{35,32}... | collective-permute-start | bytes 786440 | tf_op jit(solution)/shard_map/ppermute | solution.py:233
  31.0 4.1 %collective-permute-done.7.refs_3_ = bf16[2,256,256]{2,1,0:T(8,128)(2,1)S(1)} collective-permute-done((bf16[2,256,256]{2,1,0:T(8,128)(2,1)S(1)}, bf16[2,256,256]{2,1,0:T(8,128)(2,1)S(1)}, u32[]{:S(2)}, u32[]{:S(2)}) %collective-permute-start.7) | collective-permute-done | bytes 262176 | tf_op jit(solution)/shard_map/ppermute | solution.py:223
  35.0 0.0 collective-permute-done.9.refs_4_
  35.0 0.0 slice-start.1
  35.0 1.1 %shard_map.101 = (f32[2,2,1,1024]{3,2,1,0:T(1,128)S(1)}, f32[2,2,144,1024]{3,2,1,0:T(8,128)S(1)}) custom-call(s32[10]{0:T(128)} %refs_0_.5, bf16[16,128,256]{2,1,0:T(8,128)(2,1)S(1)} %q_kernel.1.refs_1_, bf16[2,256,256]{2,1,0:T(8,128)(2,1)S(1)} %collective-permute-done.5.refs_2_, bf16[2,256,256]{2,1,0:T(8,128)(2,1)S(1)} %collective-permute-done.7.refs_3_, ...), custom_call_target="tpu_custom_call" | custom-call | flops 6000000000 | bytes 6000000 | tf_op jit(solution)/shard_map/pallas_call | solution.py:308
  36.2 0.0 collective-permute-done.1.refs_2_
  36.2 0.0 collective-permute-done.2.refs_3_
  36.2 2.0 %collective-permute-done.3.refs_4_ = bf16[2,256,256]{2,1,0:T(8,128)(2,1)S(1)} collective-permute-done((bf16[2,256,256]{2,1,0:T(8,128)(2,1)S(1)}, bf16[2,256,256]{2,1,0:T(8,128)(2,1)S(1)}, u32[]{:S(2)}, u32[]{:S(2)}) %collective-permute-start.3) | collective-permute-done | bytes 262176 | tf_op jit(solution)/shard_map/ppermute | solution.py:233
  38.2 0.0 slice-done
  38.2 0.0 slice-done.1
  38.2 3.6 %attend_far.1 = (bf16[256,1024]{1,0:T(8,128)(2,1)S(1)}, f32[256,1024]{1,0:T(8,128)S(1)}) custom-call(s32[10]{0:T(128)} %refs_0_.5, bf16[16,128,256]{2,1,0:T(8,128)(2,1)S(1)} %q_kernel.1.refs_1_, bf16[2,256,256]{2,1,0:T(8,128)(2,1)S(1)} %collective-permute-done.1.refs_2_, bf16[2,256,256]{2,1,0:T(8,128)(2,1)S(1)} %collective-permute-done.2.refs_3_, ...), custom_call_target="tpu_custom_call" | custom-call | flops 8999999488 | bytes 14000000 | tf_op jit(solution)/shard_map/attend_far/pallas_call | solution.py:324
  41.8 7.1 %collective-permute-start.10 = (bf16[256,1024]{1,0:T(8,128)(2,1)S(1)}, bf16[256,1024]{1,0:T(8,128)(2,1)S(1)}, u32[]{:S(2)}, u32[]{:S(2)}) collective-permute-start(bf16[256,1024]{1,0:T(8,128)(2,1)S(1)} %get-tuple-element.24), channel_id=1, source_target_pairs={{0,64},{64,0},{1,65},{65,1},{2,66},{66,2},{3,67},{67,3},{4,68},{68... | collective-permute-start | bytes 1572872 | tf_op jit(solution)/shard_map/ppermute | solution.py:343
  48.9 1.5 %collective-permute-done.10 = bf16[256,1024]{1,0:T(8,128)(2,1)S(1)} collective-permute-done((bf16[256,1024]{1,0:T(8,128)(2,1)S(1)}, bf16[256,1024]{1,0:T(8,128)(2,1)S(1)}, u32[]{:S(2)}, u32[]{:S(2)}) %collective-permute-start.10) | collective-permute-done | bytes 524320 | tf_op jit(solution)/shard_map/ppermute | solution.py:343
  50.5 0.9 %add_convert_fusion = bf16[256,1024]{1,0:T(8,128)(2,1)} fusion(f32[256,1024]{1,0:T(8,128)S(1)} %get-tuple-element.23, bf16[256,1024]{1,0:T(8,128)(2,1)S(1)} %collective-permute-done.10), kind=kLoop, calls=%fused_computation | loop fusion | flops 786432 | bytes 2097152 | tf_op jit(solution)/shard_map/convert_element_type | solution.py:344
  (2 shorter events, 0.0 us)
Async XLA Ops:
  3.9 12.9 %collective-permute-start = (bf16[2,256,256]{2,1,0:T(8,128)(2,1)S(1)}, bf16[2,256,256]{2,1,0:T(8,128)(2,1)S(1)}, u32[]{:S(2)}, u32[]{:S(2)}) collective-permute-start(bf16[2,256,256]{2,1,0:T(8,128)(2,1)S(1)} %get-tuple-element.18.refs_6_), channel_id=1, source_target_pairs={{0,8},{1,9},{2,10},{3,11},{4,12},{5,13},{6,14},{7,15},{8,16},{9,17... | collective-permute-start | bytes 786440 | tf_op jit(solution)/shard_map/ppermute | solution.py:223
  7.6 13.3 %collective-permute-start.4 = (bf16[2,256,256]{2,1,0:T(8,128)(2,1)S(1)}, bf16[2,256,256]{2,1,0:T(8,128)(2,1)S(1)}, u32[]{:S(2)}, u32[]{:S(2)}) collective-permute-start(bf16[2,256,256]{2,1,0:T(8,128)(2,1)S(1)} %get-tuple-element.18.refs_6_), channel_id=1, source_target_pairs={{0,1},{1,2},{2,3},{3,0},{4,5},{5,6},{6,7},{7,4},{8,9},{9,10},{10,1... | collective-permute-start | bytes 786440 | tf_op jit(solution)/shard_map/ppermute | solution.py:233
  9.2 12.7 %collective-permute-start.6 = (bf16[2,256,256]{2,1,0:T(8,128)(2,1)S(1)}, bf16[2,256,256]{2,1,0:T(8,128)(2,1)S(1)}, u32[]{:S(2)}, u32[]{:S(2)}) collective-permute-start(bf16[2,256,256]{2,1,0:T(8,128)(2,1)S(1)} %get-tuple-element.18.refs_6_), channel_id=1, source_target_pairs={{0,3},{1,0},{2,1},{3,2},{4,7},{5,4},{6,5},{7,6},{8,11},{9,8},{10,9... | collective-permute-start | bytes 786440 | tf_op jit(solution)/shard_map/ppermute | solution.py:233
  11.3 10.7 %collective-permute-start.8 = (bf16[2,256,256]{2,1,0:T(8,128)(2,1)S(1)}, bf16[2,256,256]{2,1,0:T(8,128)(2,1)S(1)}, u32[]{:S(2)}, u32[]{:S(2)}) collective-permute-start(bf16[2,256,256]{2,1,0:T(8,128)(2,1)S(1)} %get-tuple-element.18.refs_6_), channel_id=1, source_target_pairs={{0,4},{1,5},{2,6},{3,7},{4,8},{5,9},{6,10},{7,11},{8,12},{9,13},{1... | collective-permute-start | bytes 786440 | tf_op jit(solution)/shard_map/ppermute | solution.py:223
  16.9 19.3 %collective-permute-start.1 = (bf16[2,256,256]{2,1,0:T(8,128)(2,1)S(1)}, bf16[2,256,256]{2,1,0:T(8,128)(2,1)S(1)}, u32[]{:S(2)}, u32[]{:S(2)}) collective-permute-start(bf16[2,256,256]{2,1,0:T(8,128)(2,1)S(1)} %broadcast_select_fusion), channel_id=1, source_target_pairs={{0,2},{1,3},{2,0},{3,1},{4,6},{5,7},{6,4},{7,5},{8,10},{9,11},{10,... | collective-permute-start | bytes 786440 | tf_op jit(solution)/shard_map/ppermute | solution.py:233
  19.6 16.6 %collective-permute-start.2 = (bf16[2,256,256]{2,1,0:T(8,128)(2,1)S(1)}, bf16[2,256,256]{2,1,0:T(8,128)(2,1)S(1)}, u32[]{:S(2)}, u32[]{:S(2)}) collective-permute-start(bf16[2,256,256]{2,1,0:T(8,128)(2,1)S(1)} %collective-permute-done.refs_5_), channel_id=1, source_target_pairs={{1,0},{2,1},{3,2},{5,4},{6,5},{7,6},{9,8},{10,9},{11,10},{13,12},{... | collective-permute-start | bytes 786440 | tf_op jit(solution)/shard_map/ppermute | solution.py:233
  20.9 8.6 %collective-permute-start.5 = (bf16[2,256,256]{2,1,0:T(8,128)(2,1)S(1)}, bf16[2,256,256]{2,1,0:T(8,128)(2,1)S(1)}, u32[]{:S(2)}, u32[]{:S(2)}) collective-permute-start(bf16[2,256,256]{2,1,0:T(8,128)(2,1)S(1)} %collective-permute-done.4.refs_3_), channel_id=1, source_target_pairs={{0,4},{1,5},{2,6},{3,7},{4,8},{5,9},{6,10},{7,11},{8,12},{9,13},{1... | collective-permute-start | bytes 786440 | tf_op jit(solution)/shard_map/ppermute | solution.py:223
  21.9 13.1 %collective-permute-start.7 = (bf16[2,256,256]{2,1,0:T(8,128)(2,1)S(1)}, bf16[2,256,256]{2,1,0:T(8,128)(2,1)S(1)}, u32[]{:S(2)}, u32[]{:S(2)}) collective-permute-start(bf16[2,256,256]{2,1,0:T(8,128)(2,1)S(1)} %collective-permute-done.6.refs_4_), channel_id=1, source_target_pairs={{0,4},{1,5},{2,6},{3,7},{4,8},{5,9},{6,10},{7,11},{8,12},{9,13},{1... | collective-permute-start | bytes 786440 | tf_op jit(solution)/shard_map/ppermute | solution.py:223
  22.0 13.0 %collective-permute-start.9 = (bf16[2,256,256]{2,1,0:T(8,128)(2,1)S(1)}, bf16[2,256,256]{2,1,0:T(8,128)(2,1)S(1)}, u32[]{:S(2)}, u32[]{:S(2)}) collective-permute-start(bf16[2,256,256]{2,1,0:T(8,128)(2,1)S(1)} %collective-permute-done.8.refs_2_), channel_id=1, source_target_pairs={{0,2},{1,3},{2,0},{3,1},{4,6},{5,7},{6,4},{7,5},{8,10},{9,11},{10,... | collective-permute-start | bytes 786440 | tf_op jit(solution)/shard_map/ppermute | solution.py:233
  25.5 12.7 %slice-start = ((s8[8388608]{0:T(1024)(128)(4,1)}), s8[4194304]{0:T(1024)(128)(4,1)S(1)}, s32[]{:S(2)}) async-start(s8[8388608]{0:T(1024)(128)(4,1)} %bitcast.3), calls=%async_computation | async-start | bytes 8388608
  29.5 8.7 %collective-permute-start.3 = (bf16[2,256,256]{2,1,0:T(8,128)(2,1)S(1)}, bf16[2,256,256]{2,1,0:T(8,128)(2,1)S(1)}, u32[]{:S(2)}, u32[]{:S(2)}) collective-permute-start(bf16[2,256,256]{2,1,0:T(8,128)(2,1)S(1)} %collective-permute-done.refs_5_), channel_id=1, source_target_pairs={{3,0},{7,4},{11,8},{15,12},{19,16},{23,20},{27,24},{31,28},{35,32}... | collective-permute-start | bytes 786440 | tf_op jit(solution)/shard_map/ppermute | solution.py:233
  35.0 3.2 %slice-start.1 = ((s8[8388608]{0:T(1024)(128)(4,1)}), s8[4194304]{0:T(1024)(128)(4,1)S(1)}, s32[]{:S(2)}) async-start(s8[8388608]{0:T(1024)(128)(4,1)} %bitcast.3), calls=%async_computation.1 | async-start | bytes 8388608
  41.8 8.7 %collective-permute-start.10 = (bf16[256,1024]{1,0:T(8,128)(2,1)S(1)}, bf16[256,1024]{1,0:T(8,128)(2,1)S(1)}, u32[]{:S(2)}, u32[]{:S(2)}) collective-permute-start(bf16[256,1024]{1,0:T(8,128)(2,1)S(1)} %get-tuple-element.24), channel_id=1, source_target_pairs={{0,64},{64,0},{1,65},{65,1},{2,66},{66,2},{3,67},{67,3},{4,68},{68... | collective-permute-start | bytes 1572872 | tf_op jit(solution)/shard_map/ppermute | solution.py:343
where the time goes:
time: 51.6 us; the launch traced here: 51.4 us
  starting transfers between devices  24.9 us (48%)
  Pallas kernels  16.5 us (32%)
  waiting for transfers between devices  8.92 us (17%)
  other arithmetic  0.97 us (2%)
    ppermute x6, starting transfers between devices, moved(): return lax.ppermute(value, 'tok', pairs)  12.7 us
    ppermute x1, starting transfers between devices, layer(): other = lax.ppermute(send, 'role', [(0, 1), (1, 0)])  7.14 us
    ppermute x4, waiting for transfers between devices, shifted(): lax.ppermute(value, 'tok', [(t, (t + by) % peers) for t in range(peers)])  5.37 us
    pallas_call x1, Pallas kernels, layer(): pl.pallas_call(q_kernel, out_shape=jax.ShapeDtypeStruct((hq, HD, TOK), BF...  5.15 us
    ppermute x4, starting transfers between devices, shifted(): lax.ppermute(value, 'tok', [(t, (t + by) % peers) for t in range(peers)])  5.09 us
    pallas_call x1, Pallas kernels, layer(): pl.pallas_call(kv_kernel, out_shape=(jax.ShapeDtypeStruct((TOK, d), BF),...  3.93 us
    pallas_call x2, Pallas kernels, stage(): pl.pallas_call(functools.partial(attend_kernel, table, extra, False), out...  3.81 us
    pallas_call x1, Pallas kernels, layer(): pl.pallas_call(functools.partial(attend_kernel, FAR, False, True), out_sh...  3.57 us
  transfers between devices with their start and end apart: 11, of which 4 were waited for; matrix products, arithmetic and copies ran while one was open for 0% of the time, Pallas kernels for 17%

commit v1 on v0

--- a/solution.py
+++ b/solution.py
@@ -125,7 +125,7 @@
         refs = refs[2:]
     if last_stage:
         wout, refs = refs[0], refs[1:]
-        send_o, keep_o, win, hops, m_s, acc_s, att = refs
+        send_o, att, win, hops, m_s, acc_s = refs
     else:
         m_s, acc_s, win, hops = refs
     sources = pieces + ([own] if first_stage else [])
@@ -206,11 +206,15 @@
                     att[i * BLK:(i + 1) * BLK, (g * 8 + h) * HD:(g * 8 + h + 1) * HD] = o.T.astype(BF)
     if last_stage:
         half = wout.shape[1] // 2
-        a = att[...]
         theirs = pl.multiple_of((1 - role) * half, half)
-        mine = pl.multiple_of(role * half, half)
-        send_o[...] = jnp.dot(a, wout[:, pl.ds(theirs, half)], preferred_element_type=F32).astype(BF)
-        keep_o[...] = jnp.dot(a, wout[:, pl.ds(mine, half)], preferred_element_type=F32)
+        send_o[...] = jnp.dot(
+            att[...], wout[:, pl.ds(theirs, half)], preferred_element_type=F32).astype(BF)
+
+
+def keep_kernel(att, wout, keep_o):
+    half = wout.shape[1] // 2
+    mine = pl.multiple_of(lax.axis_index("role") * half, half)
+    keep_o[...] = jnp.dot(att[...], wout[:, pl.ds(mine, half)], preferred_element_type=F32)
 
 
 HBM = pl.BlockSpec(memory_space=pltpu.MemorySpace.HBM)
@@ -321,11 +325,11 @@
     partial = stage(NEAR, [row1, up1, down1, row2, kv], True)
     partial = stage(MID, [*mid, *partial], False)
     half = w_out.shape[1] // 2
-    send, keep = pl.pallas_call(
+    send, att = pl.pallas_call(
         functools.partial(attend_kernel, FAR, False, True),
         out_shape=(
             jax.ShapeDtypeStruct((TOK, half), BF),
-            jax.ShapeDtypeStruct((TOK, half), F32),
+            jax.ShapeDtypeStruct((TOK, hq * HD), BF),
         ),
         in_specs=[SMEM] + [VM] * (len(FAR) + 4),
         out_specs=[VM, VM],
@@ -334,13 +338,21 @@
             pltpu.SMEM((len(FAR),), jnp.int32),
             pltpu.VMEM(state[0].shape, F32),
             pltpu.VMEM(state[1].shape, F32),
-            pltpu.VMEM((TOK, hq * HD), BF),
         ],
         cost_estimate=pl.CostEstimate(flops=9_000_000_000, transcendentals=0, bytes_accessed=14_000_000),
         name="attend_far",
         compiler_params=pltpu.CompilerParams(vmem_limit_bytes=28 << 20),
     )(doc_blocks, queries, *far, *partial, w_out)
     other = lax.ppermute(send, "role", [(0, 1), (1, 0)])
+    keep = pl.pallas_call(
+        keep_kernel,
+        out_shape=jax.ShapeDtypeStruct((TOK, half), F32),
+        in_specs=[VM, VM],
+        out_specs=VM,
+        cost_estimate=pl.CostEstimate(flops=2_000_000_000, transcendentals=0, bytes_accessed=6_000_000),
+        name="keep_kernel",
+        compiler_params=pltpu.CompilerParams(vmem_limit_bytes=12 << 20),
+    )(att, w_out)
     return (keep + other.astype(F32)).astype(BF)
 
 

time: 51.6 us -> 50.5 us (0.979)
  waiting for transfers between devices: 8.92 us -> 7.68 us
    ppermute x1, waiting for transfers between devices: 1.54 us -> 0.29 us  [layer(): other = lax.ppermute(send, 'role', [(0, 1), (1, 0)])]
    pallas_call x0 -> x1, Pallas kernels: none -> 1.24 us  [layer(): pl.pallas_call(keep_kernel, out_shape=jax.ShapeDtypeStruct((TOK, half), F...]
    pallas_call x1, Pallas kernels: 3.57 us -> 2.49 us  [layer(): pl.pallas_call(functools.partial(attend_kernel, FAR, False, True), out_sh...]
  transfers between devices with their start and end apart: 11 -> 11, of which waited for: 4 -> 4; matrix products, arithmetic and copies ran while one was open for 0% -> 0% of each run, Pallas kernels for 17% -> 20%
where the time goes in v1:
time: 50.5 us; the launch traced here: 50.3 us
  starting transfers between devices  24.9 us (49%)
  Pallas kernels  16.6 us (33%)
  waiting for transfers between devices  7.68 us (15%)
  other arithmetic  0.97 us (2%)
    ppermute x6, starting transfers between devices, moved(): return lax.ppermute(value, 'tok', pairs)  12.7 us
    ppermute x1, starting transfers between devices, layer(): other = lax.ppermute(send, 'role', [(0, 1), (1, 0)])  7.15 us
    ppermute x4, waiting for transfers between devices, shifted(): lax.ppermute(value, 'tok', [(t, (t + by) % peers) for t in range(peers)])  5.37 us
    pallas_call x1, Pallas kernels, layer(): pl.pallas_call(q_kernel, out_shape=jax.ShapeDtypeStruct((hq, HD, TOK), BF...  5.15 us
    ppermute x4, starting transfers between devices, shifted(): lax.ppermute(value, 'tok', [(t, (t + by) % peers) for t in range(peers)])  5.09 us
    pallas_call x1, Pallas kernels, layer(): pl.pallas_call(kv_kernel, out_shape=(jax.ShapeDtypeStruct((TOK, d), BF),...  3.93 us
    pallas_call x2, Pallas kernels, stage(): pl.pallas_call(functools.partial(attend_kernel, table, extra, False), out...  3.81 us
    pallas_call x1, Pallas kernels, layer(): pl.pallas_call(functools.partial(attend_kernel, FAR, False, True), out_sh...  2.49 us
  transfers between devices with their start and end apart: 11, of which 4 were waited for; matrix products, arithmetic and copies ran while one was open for 0% of the time, Pallas kernels for 20%

profile of v1, /device:TPU:1, one launch (start us, length us, event | category | flops | bytes accessed | tf_op | source)
XLA Modules:
  0.0 50.3 jit_solution(3463034445886102292)
XLA Ops:
  0.0 3.9 %kv_kernel.1 = (bf16[256,2048]{1,0:T(8,128)(2,1)S(1)}, bf16[2,256,256]{2,1,0:T(8,128)(2,1)S(1)}, f32[128,256]{1,0:T(8,128)S(1)}, f32[128,256]{1,0:T(8,128)S(1)}) custom-call(s32[10]{0:T(128)} %refs_0_.5, bf16[256,2048]{1,0:T(8,128)(2,1)} %hid.1, f32[1,2048]{1,0:T(1,128)} %bitcast.5, bf16[2048,256]{1,0:T(8,128)(2,1)} %wk.1, bf16[2048,256]{1,0:T(8,128)(2,1)} %wv.1, ...), custom_call_target="tpu_custom_call" | custom-call | flops 540000000 | bytes 4000000 | tf_op jit(solution)/shard_map/kv_kernel/pallas_call | solution.py:253
  3.9 3.6 %collective-permute-start = (bf16[2,256,256]{2,1,0:T(8,128)(2,1)S(1)}, bf16[2,256,256]{2,1,0:T(8,128)(2,1)S(1)}, u32[]{:S(2)}, u32[]{:S(2)}) collective-permute-start(bf16[2,256,256]{2,1,0:T(8,128)(2,1)S(1)} %get-tuple-element.18.refs_6_), channel_id=1, source_target_pairs={{0,8},{1,9},{2,10},{3,11},{4,12},{5,13},{6,14},{7,15},{8,16},{9,17... | collective-permute-start | bytes 786440 | tf_op jit(solution)/shard_map/ppermute | solution.py:227
  7.6 1.6 %collective-permute-start.4 = (bf16[2,256,256]{2,1,0:T(8,128)(2,1)S(1)}, bf16[2,256,256]{2,1,0:T(8,128)(2,1)S(1)}, u32[]{:S(2)}, u32[]{:S(2)}) collective-permute-start(bf16[2,256,256]{2,1,0:T(8,128)(2,1)S(1)} %get-tuple-element.18.refs_6_), channel_id=1, source_target_pairs={{0,1},{1,2},{2,3},{3,0},{4,5},{5,6},{6,7},{7,4},{8,9},{9,10},{10,1... | collective-permute-start | bytes 786440 | tf_op jit(solution)/shard_map/ppermute | solution.py:237
  9.2 2.1 %collective-permute-start.6 = (bf16[2,256,256]{2,1,0:T(8,128)(2,1)S(1)}, bf16[2,256,256]{2,1,0:T(8,128)(2,1)S(1)}, u32[]{:S(2)}, u32[]{:S(2)}) collective-permute-start(bf16[2,256,256]{2,1,0:T(8,128)(2,1)S(1)} %get-tuple-element.18.refs_6_), channel_id=1, source_target_pairs={{0,3},{1,0},{2,1},{3,2},{4,7},{5,4},{6,5},{7,6},{8,11},{9,8},{10,9... | collective-permute-start | bytes 786440 | tf_op jit(solution)/shard_map/ppermute | solution.py:237
  11.3 0.3 collective-permute-start.8
  11.6 5.1 %q_kernel.1.refs_1_ = bf16[16,128,256]{2,1,0:T(8,128)(2,1)S(1)} custom-call(bf16[256,2048]{1,0:T(8,128)(2,1)S(1)} %get-tuple-element.15.normed, bf16[2048,2048]{1,0:T(8,128)(2,1)} %wq.1, f32[1,128]{1,0:T(1,128)} %bitcast.7, f32[128,256]{1,0:T(8,128)S(1)} %get-tuple-element.16.cos, f32[128,256]{1,0:T(8,128)S(1)} %get-tuple-element.17.sin), custom_call_target="tpu_custom_call" | custom-call | flops 2147000064 | bytes 10000000 | tf_op jit(solution)/shard_map/q_kernel/pallas_call | solution.py:282
  16.8 0.0 collective-permute-done.refs_5_
  16.9 2.7 %collective-permute-start.1 = (bf16[2,256,256]{2,1,0:T(8,128)(2,1)S(1)}, bf16[2,256,256]{2,1,0:T(8,128)(2,1)S(1)}, u32[]{:S(2)}, u32[]{:S(2)}) collective-permute-start(bf16[2,256,256]{2,1,0:T(8,128)(2,1)S(1)} %broadcast_select_fusion), channel_id=1, source_target_pairs={{0,2},{1,3},{2,0},{3,1},{4,6},{5,7},{6,4},{7,5},{8,10},{9,11},{10,... | collective-permute-start | bytes 786440 | tf_op jit(solution)/shard_map/ppermute | solution.py:237
  19.6 1.3 %collective-permute-start.2 = (bf16[2,256,256]{2,1,0:T(8,128)(2,1)S(1)}, bf16[2,256,256]{2,1,0:T(8,128)(2,1)S(1)}, u32[]{:S(2)}, u32[]{:S(2)}) collective-permute-start(bf16[2,256,256]{2,1,0:T(8,128)(2,1)S(1)} %collective-permute-done.refs_5_), channel_id=1, source_target_pairs={{1,0},{2,1},{3,2},{5,4},{6,5},{7,6},{9,8},{10,9},{11,10},{13,12},{... | collective-permute-start | bytes 786440 | tf_op jit(solution)/shard_map/ppermute | solution.py:237
  20.9 0.0 collective-permute-done.4.refs_3_
  20.9 1.0 %collective-permute-start.5 = (bf16[2,256,256]{2,1,0:T(8,128)(2,1)S(1)}, bf16[2,256,256]{2,1,0:T(8,128)(2,1)S(1)}, u32[]{:S(2)}, u32[]{:S(2)}) collective-permute-start(bf16[2,256,256]{2,1,0:T(8,128)(2,1)S(1)} %collective-permute-done.4.refs_3_), channel_id=1, source_target_pairs={{0,4},{1,5},{2,6},{3,7},{4,8},{5,9},{6,10},{7,11},{8,12},{9,13},{1... | collective-permute-start | bytes 786440 | tf_op jit(solution)/shard_map/ppermute | solution.py:227
  21.9 0.0 collective-permute-done.6.refs_4_
  21.9 0.1 collective-permute-start.7
  22.0 0.0 collective-permute-done.8.refs_2_
  22.0 3.5 %collective-permute-start.9 = (bf16[2,256,256]{2,1,0:T(8,128)(2,1)S(1)}, bf16[2,256,256]{2,1,0:T(8,128)(2,1)S(1)}, u32[]{:S(2)}, u32[]{:S(2)}) collective-permute-start(bf16[2,256,256]{2,1,0:T(8,128)(2,1)S(1)} %collective-permute-done.8.refs_2_), channel_id=1, source_target_pairs={{0,2},{1,3},{2,0},{3,1},{4,6},{5,7},{6,4},{7,5},{8,10},{9,11},{10,... | collective-permute-start | bytes 786440 | tf_op jit(solution)/shard_map/ppermute | solution.py:237
  25.5 0.0 slice-start
  25.5 2.7 %shard_map.100 = (f32[2,2,1,1024]{3,2,1,0:T(1,128)S(1)}, f32[2,2,144,1024]{3,2,1,0:T(8,128)S(1)}) custom-call(s32[10]{0:T(128)} %refs_0_.5, bf16[16,128,256]{2,1,0:T(8,128)(2,1)S(1)} %q_kernel.1.refs_1_, bf16[2,256,256]{2,1,0:T(8,128)(2,1)S(1)} %collective-permute-done.8.refs_2_, bf16[2,256,256]{2,1,0:T(8,128)(2,1)S(1)} %collective-permute-done.4.refs_3_, ...), custom_call_target="tpu_custom_call" | custom-call | flops 6000000000 | bytes 6000000 | tf_op jit(solution)/shard_map/pallas_call | solution.py:312
  28.2 1.3 %collective-permute-done.5.refs_2_ = bf16[2,256,256]{2,1,0:T(8,128)(2,1)S(1)} collective-permute-done((bf16[2,256,256]{2,1,0:T(8,128)(2,1)S(1)}, bf16[2,256,256]{2,1,0:T(8,128)(2,1)S(1)}, u32[]{:S(2)}, u32[]{:S(2)}) %collective-permute-start.5) | collective-permute-done | bytes 262176 | tf_op jit(solution)/shard_map/ppermute | solution.py:227
  29.5 1.5 %collective-permute-start.3 = (bf16[2,256,256]{2,1,0:T(8,128)(2,1)S(1)}, bf16[2,256,256]{2,1,0:T(8,128)(2,1)S(1)}, u32[]{:S(2)}, u32[]{:S(2)}) collective-permute-start(bf16[2,256,256]{2,1,0:T(8,128)(2,1)S(1)} %collective-permute-done.refs_5_), channel_id=1, source_target_pairs={{3,0},{7,4},{11,8},{15,12},{19,16},{23,20},{27,24},{31,28},{35,32}... | collective-permute-start | bytes 786440 | tf_op jit(solution)/shard_map/ppermute | solution.py:237
  31.0 4.1 %collective-permute-done.7.refs_3_ = bf16[2,256,256]{2,1,0:T(8,128)(2,1)S(1)} collective-permute-done((bf16[2,256,256]{2,1,0:T(8,128)(2,1)S(1)}, bf16[2,256,256]{2,1,0:T(8,128)(2,1)S(1)}, u32[]{:S(2)}, u32[]{:S(2)}) %collective-permute-start.7) | collective-permute-done | bytes 262176 | tf_op jit(solution)/shard_map/ppermute | solution.py:227
  35.0 0.0 collective-permute-done.9.refs_4_
  35.0 1.1 %shard_map.101 = (f32[2,2,1,1024]{3,2,1,0:T(1,128)S(1)}, f32[2,2,144,1024]{3,2,1,0:T(8,128)S(1)}) custom-call(s32[10]{0:T(128)} %refs_0_.5, bf16[16,128,256]{2,1,0:T(8,128)(2,1)S(1)} %q_kernel.1.refs_1_, bf16[2,256,256]{2,1,0:T(8,128)(2,1)S(1)} %collective-permute-done.5.refs_2_, bf16[2,256,256]{2,1,0:T(8,128)(2,1)S(1)} %collective-permute-done.7.refs_3_, ...), custom_call_target="tpu_custom_call" | custom-call | flops 6000000000 | bytes 6000000 | tf_op jit(solution)/shard_map/pallas_call | solution.py:312
  36.2 0.0 collective-permute-done.1.refs_2_
  36.2 0.0 collective-permute-done.2.refs_3_
  36.2 2.0 %collective-permute-done.3.refs_4_ = bf16[2,256,256]{2,1,0:T(8,128)(2,1)S(1)} collective-permute-done((bf16[2,256,256]{2,1,0:T(8,128)(2,1)S(1)}, bf16[2,256,256]{2,1,0:T(8,128)(2,1)S(1)}, u32[]{:S(2)}, u32[]{:S(2)}) %collective-permute-start.3) | collective-permute-done | bytes 262176 | tf_op jit(solution)/shard_map/ppermute | solution.py:237
  38.2 0.0 slice-done
  38.2 0.0 slice-done.1
  38.2 2.5 %attend_far.1 = (bf16[256,1024]{1,0:T(8,128)(2,1)S(1)}, bf16[256,2048]{1,0:T(8,128)(2,1)S(1)}) custom-call(s32[10]{0:T(128)} %refs_0_.5, bf16[16,128,256]{2,1,0:T(8,128)(2,1)S(1)} %q_kernel.1.refs_1_, bf16[2,256,256]{2,1,0:T(8,128)(2,1)S(1)} %collective-permute-done.1.refs_2_, bf16[2,256,256]{2,1,0:T(8,128)(2,1)S(1)} %collective-permute-done.2.refs_3_, ...), custom_call_target="tpu_custom_call" | custom-call | flops 8999999488 | bytes 14000000 | tf_op jit(solution)/shard_map/attend_far/pallas_call | solution.py:328
  40.7 7.2 %collective-permute-start.10 = (bf16[256,1024]{1,0:T(8,128)(2,1)S(1)}, bf16[256,1024]{1,0:T(8,128)(2,1)S(1)}, u32[]{:S(2)}, u32[]{:S(2)}) collective-permute-start(bf16[256,1024]{1,0:T(8,128)(2,1)S(1)} %get-tuple-element.24), channel_id=1, source_target_pairs={{0,64},{64,0},{1,65},{65,1},{2,66},{66,2},{3,67},{67,3},{4,68},{68... | collective-permute-start | bytes 1572872 | tf_op jit(solution)/shard_map/ppermute | solution.py:346
  47.9 1.2 %keep_kernel.1 = f32[256,1024]{1,0:T(8,128)S(1)} custom-call(bf16[256,2048]{1,0:T(8,128)(2,1)S(1)} %get-tuple-element.23.att, bf16[2048,2048]{1,0:T(8,128)(2,1)S(1)} %bitcast.4), custom_call_target="tpu_custom_call" | custom-call | flops 2000000000 | bytes 6000000 | tf_op jit(solution)/shard_map/keep_kernel/pallas_call | solution.py:347
  49.1 0.3 collective-permute-done.10
  49.4 0.9 %add_convert_fusion = bf16[256,1024]{1,0:T(8,128)(2,1)} fusion(f32[256,1024]{1,0:T(8,128)S(1)} %keep_kernel.1, bf16[256,1024]{1,0:T(8,128)(2,1)S(1)} %collective-permute-done.10), kind=kLoop, calls=%fused_computation | loop fusion | flops 786432 | bytes 2097152 | tf_op jit(solution)/shard_map/convert_element_type | solution.py:356
  (3 shorter events, 0.0 us)
Async XLA Ops:
  3.9 12.9 %collective-permute-start = (bf16[2,256,256]{2,1,0:T(8,128)(2,1)S(1)}, bf16[2,256,256]{2,1,0:T(8,128)(2,1)S(1)}, u32[]{:S(2)}, u32[]{:S(2)}) collective-permute-start(bf16[2,256,256]{2,1,0:T(8,128)(2,1)S(1)} %get-tuple-element.18.refs_6_), channel_id=1, source_target_pairs={{0,8},{1,9},{2,10},{3,11},{4,12},{5,13},{6,14},{7,15},{8,16},{9,17... | collective-permute-start | bytes 786440 | tf_op jit(solution)/shard_map/ppermute | solution.py:227
  7.6 13.3 %collective-permute-start.4 = (bf16[2,256,256]{2,1,0:T(8,128)(2,1)S(1)}, bf16[2,256,256]{2,1,0:T(8,128)(2,1)S(1)}, u32[]{:S(2)}, u32[]{:S(2)}) collective-permute-start(bf16[2,256,256]{2,1,0:T(8,128)(2,1)S(1)} %get-tuple-element.18.refs_6_), channel_id=1, source_target_pairs={{0,1},{1,2},{2,3},{3,0},{4,5},{5,6},{6,7},{7,4},{8,9},{9,10},{10,1... | collective-permute-start | bytes 786440 | tf_op jit(solution)/shard_map/ppermute | solution.py:237
  9.2 12.7 %collective-permute-start.6 = (bf16[2,256,256]{2,1,0:T(8,128)(2,1)S(1)}, bf16[2,256,256]{2,1,0:T(8,128)(2,1)S(1)}, u32[]{:S(2)}, u32[]{:S(2)}) collective-permute-start(bf16[2,256,256]{2,1,0:T(8,128)(2,1)S(1)} %get-tuple-element.18.refs_6_), channel_id=1, source_target_pairs={{0,3},{1,0},{2,1},{3,2},{4,7},{5,4},{6,5},{7,6},{8,11},{9,8},{10,9... | collective-permute-start | bytes 786440 | tf_op jit(solution)/shard_map/ppermute | solution.py:237
  11.3 10.7 %collective-permute-start.8 = (bf16[2,256,256]{2,1,0:T(8,128)(2,1)S(1)}, bf16[2,256,256]{2,1,0:T(8,128)(2,1)S(1)}, u32[]{:S(2)}, u32[]{:S(2)}) collective-permute-start(bf16[2,256,256]{2,1,0:T(8,128)(2,1)S(1)} %get-tuple-element.18.refs_6_), channel_id=1, source_target_pairs={{0,4},{1,5},{2,6},{3,7},{4,8},{5,9},{6,10},{7,11},{8,12},{9,13},{1... | collective-permute-start | bytes 786440 | tf_op jit(solution)/shard_map/ppermute | solution.py:227
  16.9 19.3 %collective-permute-start.1 = (bf16[2,256,256]{2,1,0:T(8,128)(2,1)S(1)}, bf16[2,256,256]{2,1,0:T(8,128)(2,1)S(1)}, u32[]{:S(2)}, u32[]{:S(2)}) collective-permute-start(bf16[2,256,256]{2,1,0:T(8,128)(2,1)S(1)} %broadcast_select_fusion), channel_id=1, source_target_pairs={{0,2},{1,3},{2,0},{3,1},{4,6},{5,7},{6,4},{7,5},{8,10},{9,11},{10,... | collective-permute-start | bytes 786440 | tf_op jit(solution)/shard_map/ppermute | solution.py:237
  19.6 16.6 %collective-permute-start.2 = (bf16[2,256,256]{2,1,0:T(8,128)(2,1)S(1)}, bf16[2,256,256]{2,1,0:T(8,128)(2,1)S(1)}, u32[]{:S(2)}, u32[]{:S(2)}) collective-permute-start(bf16[2,256,256]{2,1,0:T(8,128)(2,1)S(1)} %collective-permute-done.refs_5_), channel_id=1, source_target_pairs={{1,0},{2,1},{3,2},{5,4},{6,5},{7,6},{9,8},{10,9},{11,10},{13,12},{... | collective-permute-start | bytes 786440 | tf_op jit(solution)/shard_map/ppermute | solution.py:237
  20.9 8.6 %collective-permute-start.5 = (bf16[2,256,256]{2,1,0:T(8,128)(2,1)S(1)}, bf16[2,256,256]{2,1,0:T(8,128)(2,1)S(1)}, u32[]{:S(2)}, u32[]{:S(2)}) collective-permute-start(bf16[2,256,256]{2,1,0:T(8,128)(2,1)S(1)} %collective-permute-done.4.refs_3_), channel_id=1, source_target_pairs={{0,4},{1,5},{2,6},{3,7},{4,8},{5,9},{6,10},{7,11},{8,12},{9,13},{1... | collective-permute-start | bytes 786440 | tf_op jit(solution)/shard_map/ppermute | solution.py:227
  21.9 13.1 %collective-permute-start.7 = (bf16[2,256,256]{2,1,0:T(8,128)(2,1)S(1)}, bf16[2,256,256]{2,1,0:T(8,128)(2,1)S(1)}, u32[]{:S(2)}, u32[]{:S(2)}) collective-permute-start(bf16[2,256,256]{2,1,0:T(8,128)(2,1)S(1)} %collective-permute-done.6.refs_4_), channel_id=1, source_target_pairs={{0,4},{1,5},{2,6},{3,7},{4,8},{5,9},{6,10},{7,11},{8,12},{9,13},{1... | collective-permute-start | bytes 786440 | tf_op jit(solution)/shard_map/ppermute | solution.py:227
  22.0 13.0 %collective-permute-start.9 = (bf16[2,256,256]{2,1,0:T(8,128)(2,1)S(1)}, bf16[2,256,256]{2,1,0:T(8,128)(2,1)S(1)}, u32[]{:S(2)}, u32[]{:S(2)}) collective-permute-start(bf16[2,256,256]{2,1,0:T(8,128)(2,1)S(1)} %collective-permute-done.8.refs_2_), channel_id=1, source_target_pairs={{0,2},{1,3},{2,0},{3,1},{4,6},{5,7},{6,4},{7,5},{8,10},{9,11},{10,... | collective-permute-start | bytes 786440 | tf_op jit(solution)/shard_map/ppermute | solution.py:237
  25.5 12.7 %slice-start = ((s8[8388608]{0:T(1024)(128)(4,1)}), s8[4194304]{0:T(1024)(128)(4,1)S(1)}, s32[]{:S(2)}) async-start(s8[8388608]{0:T(1024)(128)(4,1)} %bitcast.3), calls=%async_computation | async-start | bytes 8388608
  29.5 8.7 %collective-permute-start.3 = (bf16[2,256,256]{2,1,0:T(8,128)(2,1)S(1)}, bf16[2,256,256]{2,1,0:T(8,128)(2,1)S(1)}, u32[]{:S(2)}, u32[]{:S(2)}) collective-permute-start(bf16[2,256,256]{2,1,0:T(8,128)(2,1)S(1)} %collective-permute-done.refs_5_), channel_id=1, source_target_pairs={{3,0},{7,4},{11,8},{15,12},{19,16},{23,20},{27,24},{31,28},{35,32}... | collective-permute-start | bytes 786440 | tf_op jit(solution)/shard_map/ppermute | solution.py:237
  35.0 3.2 %slice-start.1 = ((s8[8388608]{0:T(1024)(128)(4,1)}), s8[4194304]{0:T(1024)(128)(4,1)S(1)}, s32[]{:S(2)}) async-start(s8[8388608]{0:T(1024)(128)(4,1)} %bitcast.3), calls=%async_computation.1 | async-start | bytes 8388608
  40.7 8.7 %collective-permute-start.10 = (bf16[256,1024]{1,0:T(8,128)(2,1)S(1)}, bf16[256,1024]{1,0:T(8,128)(2,1)S(1)}, u32[]{:S(2)}, u32[]{:S(2)}) collective-permute-start(bf16[256,1024]{1,0:T(8,128)(2,1)S(1)} %get-tuple-element.24), channel_id=1, source_target_pairs={{0,64},{64,0},{1,65},{65,1},{2,66},{66,2},{3,67},{67,3},{4,68},{68... | collective-permute-start | bytes 1572872 | tf_op jit(solution)/shard_map/ppermute | solution.py:346
